TPU v7x, 32 devices: a whole 2x2x4 slice. The times are simulated.
32 devices in a mesh: dp: 8 (over z, x), mp: 4 (over y, core).
Axes of the slice: x: 2, y: 2, z: 4, core: 2. Of those that a mesh axis runs over, the one named last changes fastest.
Arguments:
- tokens: bfloat16 [8192, 2048], P('dp', 'mp'), may hold values from -6 to 6
- norm_gain: bfloat16 [2048], replicated, may hold values from 0.099609375 to 1.8984375
- wi_gate: bfloat16 [2048, 5120], P(None, 'mp'), may hold values from -0.125 to 0.125
- wi_linear: bfloat16 [2048, 5120], P(None, 'mp'), may hold values from -0.125 to 0.125
- wo_out: bfloat16 [5120, 2048], P('mp'), may hold values from -0.078125 to 0.078125
- task_table: float32 [8, 64], replicated, may hold values from -5 to 5
- layer_table: float32 [24, 64], replicated, may hold values from -5 to 5
- task_ids: int32 [64], P('dp'), may hold values from 0 to 7
- layer_index: int32 [1], replicated, may hold values from 0 to 23
- hyper_in: bfloat16 [128, 1024], P(None, 'mp'), may hold values from -0.5 to 0.5
- gen_down: bfloat16 [1024, 131072], P(None, ('mp', 'dp')), may hold values from -0.0078125 to 0.0078125
- gen_up: bfloat16 [1024, 131072], P(None, ('mp', 'dp')), may hold values from -0.046875 to 0.046875
Outputs:
- mixed: bfloat16 [8192, 2048], P('dp', 'mp')
All inputs are finite; a program needn't handle non-finite values.
Results may differ from a plain program's by a relative error of at most 0.019.
Values may be sent and summed in bfloat16 or wider, within the bound.
A program may use at most 128 MiB of HBM per device.

v0:
```python
import jax
import jax.numpy as jnp
from jax import lax
from jax.sharding import PartitionSpec as P

R = 64


def matmul(left, right):
    return jnp.dot(left, right, preferred_element_type=jnp.float32)


def per_device(
    tokens,
    norm_gain,
    wi_gate,
    wi_linear,
    wo_out,
    task_table,
    layer_table,
    task_ids,
    layer_index,
    hyper_in,
    gen_down,
    gen_up,
):
    task_count = task_table.shape[0]
    layer_row = jnp.take(layer_table, layer_index, axis=0)
    embed = jnp.concatenate(
        [task_table, jnp.broadcast_to(layer_row, (task_count, layer_row.shape[1]))], axis=1
    ).astype(jnp.bfloat16)
    hidden_part = jnp.maximum(matmul(embed, hyper_in), 0.0).astype(jnp.bfloat16)
    hidden = lax.all_gather(hidden_part, "mp", axis=1, tiled=True)
    every_id = lax.all_gather(task_ids, "dp", axis=0, tiled=True)
    wanted = jnp.take(hidden, every_id, axis=0)
    made = (
        matmul(wanted, gen_down).astype(jnp.bfloat16),
        matmul(wanted, gen_up).astype(jnp.bfloat16),
    )
    local_down, local_up = (
        lax.all_to_all(made[0], "dp", split_axis=0, concat_axis=1, tiled=True),
        lax.all_to_all(made[1], "dp", split_axis=0, concat_axis=1, tiled=True),
    )
    full_rows = lax.all_gather(tokens, "mp", axis=1, tiled=True)
    wide = full_rows.astype(jnp.float32)
    scale = lax.rsqrt(jnp.mean(wide * wide, axis=-1, keepdims=True) + 1e-06)
    normed = (wide * scale * norm_gain.astype(jnp.float32)).astype(jnp.bfloat16)
    gate = matmul(normed, wi_gate)
    linear = matmul(normed, wi_linear)
    act = (jax.nn.gelu(gate, approximate=True) * linear).astype(jnp.bfloat16)
    seqs_dev = task_ids.shape[0]
    tok_dev = tokens.shape[0]
    seq_len = tok_dev // seqs_dev
    partial_sums = matmul(act, wo_out)
    ffout = lax.psum_scatter(
        partial_sums.astype(jnp.bfloat16), "mp", scatter_dimension=1, tiled=True
    )
    down_block = local_down.reshape(seqs_dev, -1, R)
    up_block = local_up.reshape(seqs_dev, -1, R)
    blocks = ffout.reshape(seqs_dev, seq_len, -1)
    squeeze_part = jnp.einsum(
        "std,sdr->str", blocks, down_block, preferred_element_type=jnp.float32
    )
    squeeze_full = lax.psum(squeeze_part.astype(jnp.bfloat16), "mp").astype(jnp.float32)
    squeezed = jnp.maximum(squeeze_full, 0.0).astype(jnp.bfloat16)
    expand = jnp.einsum("str,sdr->std", squeezed, up_block, preferred_element_type=jnp.float32)
    total = tokens.astype(jnp.float32) + ffout.astype(jnp.float32) + expand.reshape(tok_dev, -1)
    return total.astype(jnp.bfloat16)


def solution(mesh):
    return jax.shard_map(
        per_device,
        mesh=mesh,
        in_specs=(
            P("dp", "mp"),
            P(),
            P(None, "mp"),
            P(None, "mp"),
            P("mp", None),
            P(),
            P(),
            P("dp"),
            P(),
            P(None, "mp"),
            P(None, ("mp", "dp")),
            P(None, ("mp", "dp")),
        ),
        out_specs=P("dp", "mp"),
        check_vma=False,
    )
```

profile of v0, /device:TPU:0, one launch (start us, length us, event | category | flops | bytes accessed | tf_op | source)
XLA Modules:
  0.0 174.6 jit_solution(7065484068272233757)
XLA Ops:
  6.5 0.0 copy-start
  6.5 0.0 all-gather.2.cloned.1.call-start
  6.5 0.7 all-gather.2.cloned.1.call-update
  7.3 0.0 reduce-scatter.2.cloned.1.call-start
  7.3 0.7 convert_element_type.45
  8.0 38.1 %all-gather.2.cloned.1.call-done = bf16[1024,2048]{1,0:T(8,128)(2,1)} async-done(((bf16[1024,512]{1,0:T(8,128)(2,1)}), bf16[1024,2048]{1,0:T(8,128)(2,1)}) %all-gather.2.cloned.1.call-update) | async-done | bytes 4194320 | tf_op jit(solution)/shard_map/all_gather | solution.py:44
  46.1 3.1 %fusion = f32[1024]{0:T(1024)S(1)} fusion(bf16[1024,2048]{1,0:T(8,128)(2,1)} %all-gather.2.cloned.1.call-done), kind=kLoop, calls=%fused_computation.3 | loop fusion | flops 6290432 | bytes 4198400 | tf_op jit(solution)/shard_map/reduce_sum | solution.py:46
  49.2 10.7 %fusion.16 = f32[1024,1280]{1,0:T(8,128)} fusion(bf16[2048,1280]{1,0:T(8,128)(2,1)} %param.14, bf16[1024,2048]{1,0:T(8,128)(2,1)} %all-gather.2.cloned.1.call-done, f32[2048]{0:T(1024)S(1)} %convert_element_type.45, f32[1024]{0:T(1024)S(1)} %add_rsqrt_fusion), kind=kOutput, calls=%fused_computation.23 | convolution fusion | flops 5377097728 | bytes 14692352 | tf_op jit(solution)/shard_map/dot_general | solution.py:10
  59.9 0.0 copy-start.3
  59.9 0.0 copy-start.5
  59.9 0.0 copy-start.4
  59.9 19.9 %convolution_convert_fusion.2 = bf16[1024,2048]{1,0:T(8,128)(2,1)} fusion(bf16[1280,2048]{1,0:T(8,128)(2,1)} %param.16, f32[1024,1280]{1,0:T(8,128)} %fusion.16, bf16[2048,1280]{1,0:T(8,128)(2,1)} %param.15, bf16[1024,2048]{1,0:T(8,128)(2,1)} %all-gather.2.cloned.1.call-done, f32[2048]{0:T(1024)S(1)} %convert_element_type.45, f32[1024]{0:T(1024)S(1)} %add_rsqrt_fusion), kind=kOutput, calls=%fused_computation.20 | convolution fusion | flops 10761011200 | bytes 24129536 | tf_op jit(solution)/shard_map/dot_general | solution.py:10
  79.8 0.0 reduce-scatter.2.cloned.1.call-update
  80.5 0.0 copy-done.3
  80.5 0.7 fusion.27
  81.2 0.1 pad.3.clone
  81.3 0.0 copy-done.5
  81.3 0.6 dynamic-slice.4
  82.6 0.0 copy-done.4
  82.6 0.2 dynamic-update-slice.1
  82.8 11.4 %all-reduce = s32[64]{0:T(128)S(1)} all-reduce(s32[64]{0:T(128)S(1)} %dynamic-update-slice.1), channel_id=1, replica_groups=mesh['dp'=8,'mp'=4] {'dp'}, use_global_device_ids=true, to_apply=%add | all-reduce | flops 64 | bytes 512
  94.2 0.0 copy-done
  94.2 0.1 fusion.18
  94.3 5.2 %all_gather.11 = bf16[8,1024]{1,0:T(8,128)(2,1)S(1)} all-gather(bf16[8,256]{1,0:T(8,128)(2,1)S(1)} %fusion.18), channel_id=1, replica_groups=mesh['dp'=8,'mp'=4] {'mp'}, dimensions={1}, use_global_device_ids=true | all-gather | bytes 20480 | tf_op jit(solution)/shard_map/all_gather | solution.py:33
  99.5 0.7 gather_fusion
  100.2 5.8 %fusion.12 = bf16[8,8,4096]{2,1,0:T(8,128)(2,1)} fusion(bf16[1024,4096]{1,0:T(8,128)(2,1)} %param.22, bf16[64,1024]{1,0:T(8,128)(2,1)S(1)} %gather_fusion, pred[64]{0:T(512)(128)(4,1)S(1)} %compare_and_fusion), kind=kOutput, calls=%fused_computation.18 | convolution fusion | flops 537198592 | bytes 9044032 | tf_op jit(solution)/shard_map/dot_general | solution.py:10
  106.1 3.5 %all-to-all-start = ((bf16[8,8,4096]{2,1,0:T(8,128)(2,1)}), bf16[8,8,4096]{2,1,0:T(8,128)(2,1)S(1)}, u32[]{:S(2)}, u32[]{:S(2)}) async-start(bf16[8,8,4096]{2,1,0:T(8,128)(2,1)} %fusion.12), calls=%async_computation.1 | async-start | bytes 1048576 | tf_op jit(solution)/shard_map/all_to_all | solution.py:41
  109.6 5.8 %fusion.13 = bf16[8,8,4096]{2,1,0:T(8,128)(2,1)} fusion(bf16[1024,4096]{1,0:T(8,128)(2,1)} %param.23, bf16[64,1024]{1,0:T(8,128)(2,1)S(1)} %gather_fusion, pred[64]{0:T(512)(128)(4,1)S(1)} %compare_and_fusion), kind=kOutput, calls=%fused_computation.19 | convolution fusion | flops 537198592 | bytes 9044032 | tf_op jit(solution)/shard_map/dot_general | solution.py:10
  115.4 9.4 %all-to-all-done = bf16[8,8,4096]{2,1,0:T(8,128)(2,1)S(1)} async-done(((bf16[8,8,4096]{2,1,0:T(8,128)(2,1)}), bf16[8,8,4096]{2,1,0:T(8,128)(2,1)S(1)}, u32[]{:S(2)}, u32[]{:S(2)}) %all-to-all-start) | async-done | bytes 524320 | tf_op jit(solution)/shard_map/all_to_all | solution.py:41
  124.8 4.3 %all-to-all-start.1 = ((bf16[8,8,4096]{2,1,0:T(8,128)(2,1)}), bf16[8,8,4096]{2,1,0:T(8,128)(2,1)}, u32[]{:S(2)}, u32[]{:S(2)}) async-start(bf16[8,8,4096]{2,1,0:T(8,128)(2,1)} %fusion.13), calls=%async_computation.2 | async-start | bytes 1048576 | tf_op jit(solution)/shard_map/all_to_all | solution.py:42
  129.1 0.0 all-reduce.3.cloned.1.call-start
  129.1 0.0 copy-start.1
  129.1 0.3 copy.16
  129.4 1.1 reshape.46
  130.6 0.0 reduce-scatter.2.cloned.1.call-done
  130.6 0.0 copy-start.2
  130.6 2.5 %convolution_convert_fusion.3 = bf16[8,128,64]{1,2,0:T(8,128)(2,1)} fusion(bf16[8,128,512]{2,1,0:T(8,128)(2,1)} %bitcast.25, bf16[8,512,64]{2,1,0:T(8,128)(2,1)S(1)} %reshape.46), kind=kOutput, calls=%fused_computation.24 | convolution fusion | flops 67174400 | bytes 1703936 | tf_op jit(solution)/shard_map/std,sdr->str/dot_general | solution.py:61
  133.1 0.0 all-reduce.3.cloned.1.call-update
  133.1 10.2 %all-to-all-done.1 = bf16[8,8,4096]{2,1,0:T(8,128)(2,1)} async-done(((bf16[8,8,4096]{2,1,0:T(8,128)(2,1)}), bf16[8,8,4096]{2,1,0:T(8,128)(2,1)}, u32[]{:S(2)}, u32[]{:S(2)}) %all-to-all-start.1) | async-done | bytes 524320 | tf_op jit(solution)/shard_map/all_to_all | solution.py:42
  143.3 2.1 %copy.18 = bf16[8,8,4096]{2,1,0:T(8,128)(2,1)} copy(bf16[8,8,4096]{2,0,1:T(8,128)(2,1)} %bitcast.8) | data formatting | bytes 1048576 | tf_op jit(solution)/shard_map/all_to_all | solution.py:42
  145.4 2.1 %reshape.47 = bf16[8,512,64]{2,1,0:T(8,128)(2,1)S(1)} reshape(bf16[8,8,4096]{2,1,0:T(8,128)(2,1)} %copy.18) | data formatting | bytes 1048576 | tf_op jit(solution)/shard_map/reshape | solution.py:59
  147.5 17.7 %all-reduce.3.cloned.1.call-done = bf16[8,128,64]{1,2,0:T(8,128)(2,1)} async-done(((bf16[8,128,64]{1,2,0:T(8,128)(2,1)}), bf16[8,128,64]{1,2,0:T(8,128)(2,1)}) %all-reduce.3.cloned.1.call-update) | async-done | bytes 131088 | tf_op jit(solution)/shard_map/psum | solution.py:64
  165.2 1.4 fusion.21
  166.6 0.0 copy-done.1
  166.6 0.0 copy-done.2
  166.6 1.4 fusion.14
  (6 shorter events, 0.0 us)
Async XLA Ops:
  6.5 87.6 %copy-start = (bf16[128,256]{1,0:T(8,128)(2,1)S(1)}, bf16[128,256]{1,0:T(8,128)(2,1)}, u32[]{:S(2)}) copy-start(bf16[128,256]{1,0:T(8,128)(2,1)} %param.21) | copy-start | bytes 196612
  6.5 39.6 %all-gather.2.cloned.1.call-start = ((), (), s32[]{:S(2)}) async-start(), calls=%async_computation.3 | async-start | bytes 5242880 | tf_op jit(solution)/shard_map/all_gather | solution.py:44
  7.3 123.3 %reduce-scatter.2.cloned.1.call-start = ((), (), s32[]{:S(2)}) async-start(), calls=%async_computation.4 | async-start | bytes 5242880 | tf_op jit(solution)/shard_map/reduce_scatter | solution.py:55
  59.9 20.6 %copy-start.3 = (f32[8,64]{1,0:T(8,128)S(1)}, f32[8,64]{1,0:T(8,128)}, u32[]{:S(2)}) copy-start(f32[8,64]{1,0:T(8,128)} %param.17) | copy-start | bytes 6148
  59.9 21.4 %copy-start.5 = (u32[32]{0:T(128)S(1)}, u32[32]{0:T(128)}, u32[]{:S(2)}) copy-start(u32[32]{0:T(128)} %constant.73) | copy-start | bytes 388
  59.9 22.7 %copy-start.4 = (s32[8]{0:T(128)S(1)}, s32[8]{0:T(128)}, u32[]{:S(2)}) copy-start(s32[8]{0:T(128)} %param.19) | copy-start | bytes 100
  106.1 18.7 %all-to-all-start = ((bf16[8,8,4096]{2,1,0:T(8,128)(2,1)}), bf16[8,8,4096]{2,1,0:T(8,128)(2,1)S(1)}, u32[]{:S(2)}, u32[]{:S(2)}) async-start(bf16[8,8,4096]{2,1,0:T(8,128)(2,1)} %fusion.12), calls=%async_computation.1 | async-start | bytes 1048576 | tf_op jit(solution)/shard_map/all_to_all | solution.py:41
  124.8 18.6 %all-to-all-start.1 = ((bf16[8,8,4096]{2,1,0:T(8,128)(2,1)}), bf16[8,8,4096]{2,1,0:T(8,128)(2,1)}, u32[]{:S(2)}, u32[]{:S(2)}) async-start(bf16[8,8,4096]{2,1,0:T(8,128)(2,1)} %fusion.13), calls=%async_computation.2 | async-start | bytes 1048576 | tf_op jit(solution)/shard_map/all_to_all | solution.py:42
  129.1 36.1 %all-reduce.3.cloned.1.call-start = ((), (), s32[]{:S(2)}) async-start(), calls=%async_computation.5 | async-start | bytes 262144 | tf_op jit(solution)/shard_map/psum | solution.py:64
  129.1 37.5 %copy-start.1 = (bf16[1024,512]{1,0:T(8,128)(2,1)S(1)}, bf16[1024,512]{1,0:T(8,128)(2,1)}, u32[]{:S(2)}) copy-start(bf16[1024,512]{1,0:T(8,128)(2,1)} %param.12) | copy-start | bytes 3145732
  130.6 36.0 %copy-start.2 = (bf16[1024,512]{1,0:T(8,128)(2,1)S(1)}, bf16[1024,512]{1,0:T(8,128)(2,1)}, u32[]{:S(2)}) copy-start(bf16[1024,512]{1,0:T(8,128)(2,1)} %reduce-scatter.2.cloned.1.call-done) | copy-start | bytes 3145732
Sparse Core Ops, SparseCore 0:
  8.9 37.1 all-gather.1
  80.0 44.3 reduce-scatter.1
  133.2 31.9 all-reduce.2
where the time goes:
time: 175 us
  waiting for transfers between devices  76.2 us (44%)
  matrix products  46.2 us (26%)
  blocking collectives  16.6 us (9%)
  between operations  14.6 us (8%)
  starting transfers between devices  7.9 us (5%)
  local copies, waits for them, and re-layouts  7.23 us (4%)
  other arithmetic  5.92 us (3%)
    dot_general x5, matrix products, matmul(): return jnp.dot(left, right, preferred_element_type=jnp.float32)  42.4 us
    all_gather x1, waiting for transfers between devices, per_device(): full_rows = lax.all_gather(tokens, 'mp', axis=1, tiled=True)  38.1 us
    psum x1, waiting for transfers between devices, per_device(): lax.psum(squeeze_part.astype(jnp.bfloat16), 'mp').astype(jnp.float32)  17.7 us
    unnamed x1, blocking collectives  11.4 us
    all_to_all x1, waiting for transfers between devices, per_device(): lax.all_to_all(made[1], 'dp', split_axis=0, concat_axis=1, tiled=True)  10.2 us
    all_to_all x1, waiting for transfers between devices, per_device(): lax.all_to_all(made[0], 'dp', split_axis=0, concat_axis=1, tiled=True)  9.39 us
    all_gather x1, blocking collectives, per_device(): hidden = lax.all_gather(hidden_part, 'mp', axis=1, tiled=True)  5.2 us
    all_to_all x1, starting transfers between devices, per_device(): lax.all_to_all(made[1], 'dp', split_axis=0, concat_axis=1, tiled=True)  4.33 us
  transfers between devices with their start and end apart: 5, of which 4 were waited for; matrix products, arithmetic and copies ran while one was open for 13% of the time, Pallas kernels for 0%

commit v1 on v0

v1 whole, which is shorter than its diff:
```python
import functools

import jax
import jax.numpy as jnp
from jax import lax
from jax.experimental import pallas as pl
from jax.experimental.pallas import tpu as pltpu
from jax.sharding import PartitionSpec as P

F32, BF16 = jnp.float32, jnp.bfloat16
LANES = 128


def matmul(left, right):
    return jnp.dot(left, right, preferred_element_type=F32)


def kernel(
    n_dp, n_mp, rank,
    ids_ref, layer_at, gain_ref, task_ref, layer_ref, hyper_ref,
    tok, w_gate, w_lin, w_out, g_down, g_up,
    out,
    x_all, wg, wl, wo, gd, gu, normed, act, hid, made_all, down, up,
    part_mine, part_away, part_got, y_out, y_got, ff_all,
    sq_mine, sq_got, sq_chip, sq_far, result,
    load_sem, out_sem,
    ag_s, ag_r, pair_s, pair_r, fw_s, fw_r, hid_s, hid_r,
    gen_s, gen_r, pt_s, pt_r, y_s, y_r, sp_s, sp_r, sf_s, sf_r,
):
    dp, mp = lax.axis_index("dp"), lax.axis_index("mp")
    chips = n_mp // 2
    core, chip = lax.rem(mp, 2), lax.div(mp, 2)
    mate = chip * 2 + 1 - core
    rows_all, feat = tok.shape
    seqs = ids_ref.shape[0]
    seq = rows_all // seqs
    steps = part_mine.shape[0]
    rows = rows_all // steps
    tasks = task_ref.shape[0]
    model = feat * n_mp

    def remote(src, dst, send, recv, to_mp=None, to_dp=None):
        return pltpu.make_async_remote_copy(
            src_ref=src, dst_ref=dst, send_sem=send, recv_sem=recv,
            device_id={"dp": dp if to_dp is None else to_dp, "mp": mp if to_mp is None else to_mp},
            device_id_type=pl.DeviceIdType.MESH,
        )

    def far(off):
        return lax.rem(chip + off, chips)

    def src_chip(off):
        return lax.rem(chip + chips - off, chips)

    own_load = pltpu.make_async_copy(tok, x_all.at[mp], load_sem.at[0])
    loads = [
        pltpu.make_async_copy(src, dst, load_sem.at[i + 1])
        for i, (src, dst) in enumerate(
            [(g_down, gd), (g_up, gu), (w_gate, wg), (w_lin, wl), (w_out, wo)]
        )
    ]
    own_load.start()
    for load in loads:
        load.start()

    barrier = pltpu.get_barrier_semaphore()
    for off in range(1, n_mp):
        pl.semaphore_signal(
            barrier, inc=1, device_id={"dp": dp, "mp": lax.rem(mp + off, n_mp)},
            device_id_type=pl.DeviceIdType.MESH,
        )
    for off in range(1, n_dp):
        pl.semaphore_signal(
            barrier, inc=1, device_id={"dp": lax.rem(dp + off, n_dp), "mp": mp},
            device_id_type=pl.DeviceIdType.MESH,
        )
    pl.semaphore_wait(barrier, n_mp + n_dp - 2)

    half = task_ref.shape[1]
    row = layer_ref[pl.ds(layer_at[0], 1), :].astype(BF16)
    row = jnp.broadcast_to(row.astype(F32), (tasks, row.shape[1])).astype(BF16)
    unit = matmul(task_ref[...].astype(BF16), hyper_ref[:half, :]) + matmul(row, hyper_ref[half:, :])
    unit = jnp.maximum(unit, 0.0)
    hid[mp] = jnp.concatenate([unit, unit], axis=0).astype(BF16)

    def hid_copy(off, block, to):
        return remote(hid.at[block], hid.at[block], hid_s.at[off - 1], hid_r.at[off - 1], to_mp=to)

    def rows_of(step):
        return pl.ds(pl.multiple_of(step * rows, rows), rows)

    def ag_copy(off, step):
        return remote(
            tok.at[rows_of(step)], x_all.at[mp, rows_of(step)],
            ag_s.at[off - 1, step], ag_r.at[off - 1, step], to_mp=far(off) * 2 + core,
        )

    def ag_in(off, step):
        block = x_all.at[src_chip(off) * 2 + core, rows_of(step)]
        return remote(block, block, ag_s.at[off - 1, step], ag_r.at[off - 1, step], to_mp=mate)

    def fw_copy(off, step, which):
        block = x_all.at[src_chip(off) * 2 + which, rows_of(step)]
        return remote(block, block, fw_s.at[off - 1, step], fw_r.at[off - 1, step], to_mp=mate)

    for off in range(1, n_mp):
        hid_copy(off, mp, lax.rem(mp + off, n_mp)).start()
    pair = remote(tok, x_all.at[mp], pair_s, pair_r, to_mp=mate)
    for off in range(1, chips):
        ag_copy(off, 0).start()
    pair.start()

    @pl.loop(1, steps)
    def _(step):
        for off in range(1, chips):
            ag_copy(off, step).start()

    for off in range(1, n_mp):
        hid_copy(off, lax.rem(mp + n_mp - off, n_mp), mp * 0 + lax.rem(mp + off, n_mp)).wait_recv()
    wide_cols = g_down.shape[1]
    tile = min(512, wide_cols)
    gen_rows = wide_cols // LANES * tasks
    deep = hid.shape[2]

    def gen_block(which, at):
        return made_all.at[which, pl.ds(pl.multiple_of(at * gen_rows, gen_rows), gen_rows)]

    def gen_copy(which, off, at, to):
        return remote(
            gen_block(which, at), gen_block(which, at),
            gen_s.at[which, off - 1], gen_r.at[which, off - 1], to_dp=to,
        )

    for which, weights in enumerate((gd, gu)):
        loads[which].wait()

        @pl.loop(0, wide_cols // tile)
        def _(i):
            cols = pl.ds(pl.multiple_of(i * tile, tile), tile)
            total = matmul(hid[0], weights[0:deep, cols])
            for block in range(1, n_mp):
                total += matmul(hid[block], weights[block * deep:(block + 1) * deep, cols])
            base = dp * gen_rows + i * (tile // LANES * tasks)
            for j in range(0, tile // LANES, 2):
                two = [total[:tasks, (j + k) * LANES:(j + k + 1) * LANES] for k in range(2)]
                at = pl.ds(pl.multiple_of(base + j * tasks, 2 * tasks), 2 * tasks)
                made_all[which, at, :] = jnp.concatenate(two, axis=0).astype(BF16)

        for off in range(1, n_dp):
            gen_copy(which, off, dp, lax.rem(dp + off, n_dp)).start()

    def forward(step):
        for off in range(1, chips):
            ag_in(off, step).wait_recv()
            fw_copy(off, step, core).start()

    forward(0)
    own_load.wait()
    pair_in = remote(x_all.at[mate], x_all.at[mate], pair_s, pair_r, to_mp=mate)
    pair_in.wait_recv()
    for load in loads[2:]:
        load.wait()

    def pt_copy(step, q):
        return remote(
            part_away.at[step, q], part_got.at[step, q], pt_s.at[step, q], pt_r.at[step, q], to_mp=mate
        )

    def y_copy(step, off):
        return remote(
            y_out.at[step, off - 1], y_got.at[step, off - 1],
            y_s.at[step, off - 1], y_r.at[step, off - 1], to_mp=far(off) * 2 + core,
        )

    sub = min(64, rows)
    units = wg.shape[1]
    ff_tile = 256 if units % 256 == 0 else units

    @pl.loop(0, steps)
    def _(step):
        for off in range(1, chips):
            fw_copy(off, step, 1 - core).wait_recv()
        gain = gain_ref[...].astype(F32)
        for r in range(0, rows, sub):
            at = pl.ds(pl.multiple_of(step * rows + r, sub), sub)
            wide = jnp.concatenate([x_all[b, at, :] for b in range(n_mp)], axis=1).astype(F32)
            mean = jnp.sum(wide * wide, axis=-1, keepdims=True) * (1.0 / model)
            normed[r:r + sub, :] = (wide * lax.rsqrt(mean + 1e-06) * gain).astype(BF16)
        for f in range(0, units, ff_tile):
            gate = matmul(normed[...], wg[:, f:f + ff_tile])
            linear = matmul(normed[...], wl[:, f:f + ff_tile])
            inner = 0.7978845608028654 * (gate + 0.044715 * (gate * gate * gate))
            act[:, f:f + ff_tile] = (0.5 * gate * (1.0 + jnp.tanh(inner)) * linear).astype(BF16)
        for q in range(chips):
            cols = pl.ds(pl.multiple_of((2 * q + 1 - core) * feat, feat), feat)
            part_away[step, q] = matmul(act[...], wo[:, cols]).astype(BF16)
            pt_copy(step, q).start()
        for q in range(chips):
            cols = pl.ds(pl.multiple_of((2 * q + core) * feat, feat), feat)
            part_mine[step, q] = matmul(act[...], wo[:, cols]).astype(BF16)

        @pl.when(step + 1 < steps)
        def _():
            forward(step + 1)

        for q in range(chips):
            pt_copy(step, q).wait_recv()
        for off in range(1, chips):
            q = far(off)
            y_out[step, off - 1] = (
                part_mine[step, q].astype(F32) + part_got[step, q].astype(F32)
            ).astype(BF16)
            y_copy(step, off).start()

    for which in range(2):
        for off in range(1, n_dp):
            gen_copy(which, off, lax.rem(dp + n_dp - off, n_dp), lax.rem(dp + off, n_dp)).wait_recv()
    fold = LANES // rank
    take = LANES // tasks
    span = take * fold
    r_at = lax.broadcasted_iota(jnp.int32, (tasks * span, LANES), 0)
    c_at = lax.broadcasted_iota(jnp.int32, (tasks * span, LANES), 1)
    f_at, t_at = lax.rem(r_at, span), lax.div(r_at, span)
    pick = (lax.div(c_at, tasks) == lax.div(f_at, fold)) & (lax.rem(c_at, tasks) == t_at)
    pick = jnp.where(pick, 1.0, 0.0).astype(BF16)
    keep = lax.div(c_at, rank) == lax.rem(f_at, fold)
    for which, dst in enumerate((down, up)):

        @pl.loop(0, feat // span)
        def _(b):
            block = made_all[which, pl.ds(pl.multiple_of(b * LANES, LANES), LANES), :]
            spread = jnp.where(keep, matmul(pick, block), 0.0).astype(BF16)
            for t in range(tasks):
                dst[t, pl.ds(pl.multiple_of(b * span, span), span), :] = spread[t * span:(t + 1) * span, :]

    lane = lax.broadcasted_iota(jnp.int32, (seq, LANES), 1)
    low = lane < rank
    per = rows // seq

    def sp_copy(step):
        return remote(sq_mine.at[step], sq_got.at[step], sp_s.at[step], sp_r.at[step], to_mp=mate)

    def sf_copy(step, off):
        return remote(
            sq_chip.at[step], sq_far.at[step, off - 1],
            sf_s.at[step, off - 1], sf_r.at[step, off - 1], to_mp=far(off) * 2 + core,
        )

    @pl.loop(0, steps)
    def _(step):
        for off in range(1, chips):
            y_copy(step, off).wait_recv()
        total = part_mine[step, chip].astype(F32) + part_got[step, chip].astype(F32)
        for off in range(1, chips):
            total += y_got[step, off - 1].astype(F32)
        ff_all[rows_of(step), :] = total.astype(BF16)
        both = []
        for s in range(per):
            at = pl.ds(pl.multiple_of(step * rows + s * seq, seq), seq)
            value = matmul(ff_all[at, :], down[ids_ref[step * per + s]])
            both.append(value + pltpu.roll(value, rank, 1))
        sq_mine[step] = jnp.where(low, both[0], both[1]).astype(BF16)
        sp_copy(step).start()
        sp_copy(step).wait_recv()
        sq_chip[step] = (sq_mine[step].astype(F32) + sq_got[step].astype(F32)).astype(BF16)
        for off in range(1, chips):
            sf_copy(step, off).start()

    def out_copy(step):
        return pltpu.make_async_copy(
            result.at[rows_of(step)], out.at[rows_of(step)], out_sem.at[step]
        )

    @pl.loop(0, steps)
    def _(step):
        for off in range(1, chips):
            sf_copy(step, off).wait_recv()
        total = sq_chip[step].astype(F32)
        for off in range(1, chips):
            total += sq_far[step, off - 1].astype(F32)
        total = jnp.maximum(total, 0.0)
        for s in range(per):
            at = pl.ds(pl.multiple_of(step * rows + s * seq, seq), seq)
            mine = jnp.where(low if s == 0 else jnp.logical_not(low), total, 0.0)
            mine = (mine + pltpu.roll(mine, rank, 1)).astype(BF16)
            expand = lax.dot_general(
                mine, up[ids_ref[step * per + s]], (((1,), (1,)), ((), ())), preferred_element_type=F32
            )
            mixed = x_all[mp, at, :].astype(F32) + ff_all[at, :].astype(F32) + expand
            result[at, :] = mixed.astype(BF16)
        out_copy(step).start()

    pair.wait_send()
    for off in range(1, n_mp):
        hid_copy(off, mp, lax.rem(mp + off, n_mp)).wait_send()
    for which in range(2):
        for off in range(1, n_dp):
            gen_copy(which, off, dp, lax.rem(dp + off, n_dp)).wait_send()

    @pl.loop(0, steps)
    def _(step):
        for off in range(1, chips):
            ag_copy(off, step).wait_send()
            fw_copy(off, step, core).wait_send()
            y_copy(step, off).wait_send()
            sf_copy(step, off).wait_send()
        for q in range(chips):
            pt_copy(step, q).wait_send()
        sp_copy(step).wait_send()
        out_copy(step).wait()


def per_device(
    n_dp, n_mp,
    tokens, norm_gain, wi_gate, wi_linear, wo_out, task_table, layer_table,
    task_ids, layer_index, hyper_in, gen_down, gen_up,
):
    rows_all, feat = tokens.shape
    seqs = task_ids.shape[0]
    seq = rows_all // seqs
    rank = gen_down.shape[1] * n_dp // feat
    per = LANES // rank
    rows = seq * per
    steps = rows_all // rows
    chips = n_mp // 2
    tasks = task_table.shape[0]
    model = feat * n_mp
    dma = pltpu.SemaphoreType.DMA
    vmem = pltpu.VMEM
    far = chips - 1
    gen_rows = feat * rank // LANES * tasks
    smem = pl.BlockSpec(memory_space=pltpu.SMEM)
    inside = pl.BlockSpec(memory_space=pltpu.VMEM)
    hbm = pl.BlockSpec(memory_space=pl.ANY)
    flops = 2 * rows_all * model * wi_gate.shape[1] * 3
    return pl.pallas_call(
        functools.partial(kernel, n_dp, n_mp, rank),
        name="adapter_ffn",
        out_shape=jax.ShapeDtypeStruct(tokens.shape, BF16),
        in_specs=[smem, smem, inside, inside, inside, inside] + [hbm] * 6,
        out_specs=hbm,
        scratch_shapes=[
            vmem((n_mp, rows_all, feat), BF16),
            vmem(wi_gate.shape, BF16),
            vmem(wi_linear.shape, BF16),
            vmem(wo_out.shape, BF16),
            vmem(gen_down.shape, BF16),
            vmem(gen_up.shape, BF16),
            vmem((rows, model), BF16),
            vmem((rows, wi_gate.shape[1]), BF16),
            vmem((n_mp, 2 * tasks, hyper_in.shape[1]), BF16),
            vmem((2, gen_rows, LANES), BF16),
            vmem((tasks, feat, LANES), BF16),
            vmem((tasks, feat, LANES), BF16),
            vmem((steps, chips, rows, feat), BF16),
            vmem((steps, chips, rows, feat), BF16),
            vmem((steps, chips, rows, feat), BF16),
            vmem((steps, far, rows, feat), BF16),
            vmem((steps, far, rows, feat), BF16),
            vmem((rows_all, feat), BF16),
            vmem((steps, seq, LANES), BF16),
            vmem((steps, seq, LANES), BF16),
            vmem((steps, seq, LANES), BF16),
            vmem((steps, far, seq, LANES), BF16),
            vmem((rows_all, feat), BF16),
            dma((6,)),
            dma((steps,)),
            dma((far, steps)), dma((far, steps)),
            dma, dma,
            dma((far, steps)), dma((far, steps)),
            dma((n_mp - 1,)), dma((n_mp - 1,)),
            dma((2, n_dp - 1)), dma((2, n_dp - 1)),
            dma((steps, chips)), dma((steps, chips)),
            dma((steps, far)), dma((steps, far)),
            dma((steps,)), dma((steps,)),
            dma((steps, far)), dma((steps, far)),
        ],
        compiler_params=pltpu.CompilerParams(
            collective_id=0, has_side_effects=True, vmem_limit_bytes=62 * 1024 * 1024
        ),
        cost_estimate=pl.CostEstimate(flops=flops, bytes_accessed=34_000_000, transcendentals=0),
    )(
        task_ids, layer_index, norm_gain.reshape(1, -1), task_table, layer_table, hyper_in,
        tokens, wi_gate, wi_linear, wo_out, gen_down, gen_up,
    )


def solution(mesh):
    return jax.shard_map(
        functools.partial(per_device, mesh.shape["dp"], mesh.shape["mp"]),
        mesh=mesh,
        in_specs=(
            P("dp", "mp"),
            P(),
            P(None, "mp"),
            P(None, "mp"),
            P("mp", None),
            P(),
            P(),
            P("dp"),
            P(),
            P(None, "mp"),
            P(None, ("mp", "dp")),
            P(None, ("mp", "dp")),
        ),
        out_specs=P("dp", "mp"),
        check_vma=False,
    )
```

time: 175 us -> 64.5 us (0.37)
  waiting for transfers between devices: 76.2 us -> 0 us
  Pallas kernels: 0 us -> 60.1 us
  matrix products: 46.2 us -> 0 us
  blocking collectives: 16.6 us -> 0 us
  between operations: 14.6 us -> 0.66 us
  starting transfers between devices: 7.9 us -> 0 us
  other arithmetic: 5.92 us -> 0 us
  local copies, waits for them, and re-layouts: 7.23 us -> 3.55 us
    pallas_call x0 -> x1, Pallas kernels: none -> 60.1 us  [per_device(): pl.pallas_call(functools.partial(kernel, n_dp, n_mp, rank), name='adapter...]
    dot_general x7 -> x0, matrix products: 46.2 us -> none  [the longest x5 42.4 us: matmul(): return jnp.dot(left, right, preferred_element_type=jnp.float32)]
    all_gather x1 -> x0, waiting for transfers between devices: 38.1 us -> none  [per_device(): full_rows = lax.all_gather(tokens, 'mp', axis=1, tiled=True)]
    all_to_all x2 -> x0, waiting for transfers between devices: 19.6 us -> none  [the longest x1 10.2 us: per_device(): lax.all_to_all(made[1], 'dp', split_axis=0, concat_axis=1, tiled=True)]
    psum x1 -> x0, waiting for transfers between devices: 17.7 us -> none  [per_device(): lax.psum(squeeze_part.astype(jnp.bfloat16), 'mp').astype(jnp.float32)]
    unnamed x1 -> x0, blocking collectives: 11.4 us -> none
    all_to_all x2 -> x0, starting transfers between devices: 7.82 us -> none  [the longest x1 4.33 us: per_device(): lax.all_to_all(made[1], 'dp', split_axis=0, concat_axis=1, tiled=True)]
    all_gather x1 -> x0, blocking collectives: 5.2 us -> none  [per_device(): hidden = lax.all_gather(hidden_part, 'mp', axis=1, tiled=True)]
  transfers between devices with their start and end apart: 5 -> 0, of which waited for: 4 -> 0; matrix products, arithmetic and copies ran while one was open for 13% -> 0% of each run, Pallas kernels for 0% -> 0%
where the time goes in v1:
time: 64.5 us; the launch traced here: 64.3 us
  Pallas kernels  60.1 us (93%)
  local copies, waits for them, and re-layouts  3.55 us (6%)
  between operations  0.66 us (1%)
    pallas_call x1, Pallas kernels, per_device(): pl.pallas_call(functools.partial(kernel, n_dp, n_mp, rank), name='adapter...  60.1 us
    unnamed x1, local copies, waits for them, and re-layouts  2.26 us
    reshape x1, local copies, waits for them, and re-layouts, per_device(): norm_gain.reshape(1, -1)  1.29 us

profile of v1, /device:TPU:0, one launch (start us, length us, event | category | flops | bytes accessed | tf_op | source)
XLA Modules:
  0.0 64.3 jit_solution(1491855352639311132)
XLA Ops:
  0.7 1.3 %reshape.3.gain_ref = bf16[1,2048]{1,0:T(2,128)(2,1)} reshape(bf16[2048]{0:T(1024)(128)(2,1)} %param.13) | data formatting | bytes 8192 | tf_op jit(solution)/shard_map/reshape | solution.py:383
  1.9 60.1 %adapter_ffn.1 = bf16[1024,512]{1,0:T(8,128)(2,1)} custom-call(s32[8]{0:T(128)} %ids_ref.1, s32[1]{0:T(128)S(6)} %copy.14.layer_at, bf16[1,2048]{1,0:T(2,128)(2,1)} %reshape.3.gain_ref, f32[8,64]{1,0:T(8,128)} %task_ref.1, f32[24,64]{1,0:T(8,128)} %layer_ref.1, bf16[128,256]{1,0:T(8,128)(2,1)} %hyper_ref.1, bf16[1024,512]{1,0:T(8,128)(2,1)} %tok.1, ...), custom_call_target="tpu_custom_call" | custom-call | flops 16106127360 | bytes 34000000 | tf_op jit(solution)/shard_map/adapter_ffn/pallas_call | solution.py:336
  62.0 2.3 %copy.15 = bf16[1024,512]{1,0:T(8,128)(2,1)} copy(bf16[1024,512]{1,0:T(8,128)(2,1)} %adapter_ffn.1) | data formatting | bytes 2097152
